TPU v7x, 32 devices: a whole 2x2x4 slice. The times are simulated.
32 devices in a mesh: row: 8 (over z, core), col: 4 (over y, x).
Axes of the slice: x: 2, y: 2, z: 4, core: 2. Of those that a mesh axis runs over, the one named last changes fastest.
Arguments:
- flow_tiles: bfloat16 [8, 8, 256, 256], P('row', 'col'), may hold values from 0.1 to 25
- tile_cols: int32 [8, 8], P('row', 'col'), may hold values from -1 to 7, as said below
- pairs: int32 [512, 2], P(('row', 'col')), may hold values from -1 to 7, as said below
Outputs:
- new_flow: float32 [8, 8, 256, 256], P('row', 'col')
Inputs may be any that keep to these rules, and one draw needn't show every extreme that they name: `tile_cols`: the stored slots of device (r, c) have distinct tile columns, each congruent to c modulo the col axis's size; tile row r stores tile column r. `pairs`: device (r, c) lists, in some order and without repeats, exactly the (k, s) for which slot s of the device is stored and M[r, k] and M[k, tile_cols[r, c * 2 + s]] are both stored tiles; its other rows are (-1, -1). Some device uses all 16 rows.
All inputs are finite; a program needn't handle non-finite values.
Results may differ from a plain program's by a relative error of at most 0.0003.
Values may be sent and summed in bfloat16 or wider, within the bound.
A program may use at most 64 MiB of HBM per device.

v0:
```python
import jax
import jax.numpy as jnp
from jax import lax
from jax.sharding import PartitionSpec as P


def block_products(
    initial, left_source, right_source, left_index, right_row, right_slot, weight, groups
):
    tile_count = weight.shape[1]
    left_index = left_index.reshape(groups, -1)
    right_row = right_row.reshape(groups, -1)
    right_slot = right_slot.reshape(groups, -1)
    weight = weight.reshape(groups, -1, tile_count)

    def block_step(carried, inputs):
        left_pick, row_pick, slot_pick, weight_block = inputs
        left_tiles = left_source[left_pick]
        right_tiles = right_source[row_pick, slot_pick]
        products = jnp.einsum(
            "pab,pbc->pac", left_tiles, right_tiles, preferred_element_type=jnp.float32
        )
        added = jnp.einsum("ps,pac->sac", weight_block, products, precision=lax.Precision.HIGHEST)
        return (carried + added, None)

    result, unused = lax.scan(block_step, initial, (left_index, right_row, right_slot, weight))
    return result


def on_device(flow_tiles, tile_cols, pairs):
    tile_count = flow_tiles.shape[1]
    tile_width = flow_tiles.shape[3]
    col_count = lax.axis_size("col")
    rows_total = lax.axis_size("row") * tile_width
    col_index = lax.axis_index("col")
    row_tiles, row_cols = (
        lax.all_gather(flow_tiles, "col", axis=1, tiled=True),
        lax.all_gather(tile_cols, "col", axis=1, tiled=True),
    )
    own_cols = tile_cols[0]
    inner_tile = pairs[:, 0]
    slot_list = pairs[:, 1]
    is_live = inner_tile >= 0
    inner_safe = jnp.maximum(inner_tile, 0)
    slot_safe = jnp.maximum(slot_list, 0)
    wanted = own_cols[slot_safe]
    left_index = jnp.argmax(row_cols[0][None, :] == inner_safe[:, None], axis=1)
    slot_ids = jnp.arange(tile_count, dtype=jnp.int32)
    weight = (is_live[:, None] & (slot_list[:, None] == slot_ids[None, :])).astype(jnp.float32)
    initial = jnp.zeros((tile_count, tile_width, tile_width), jnp.float32)
    column_tiles, column_cols = (
        lax.all_gather(flow_tiles, "row", axis=0, tiled=True),
        lax.all_gather(tile_cols, "row", axis=0, tiled=True),
    )
    right_slot = jnp.argmax(column_cols[inner_safe] == wanted[:, None], axis=1)
    expanded = block_products(
        initial, row_tiles[0], column_tiles, left_index, inner_safe, right_slot, weight, 4
    )
    inflated = expanded * expanded
    partial_sums = jnp.sum(inflated, axis=1)
    targets = col_index + col_count * slot_ids
    matches = own_cols[None, :] == targets[:, None]
    canonical = jnp.sum(jnp.where(matches[:, :, None], partial_sums[None, :, :], 0.0), axis=1)
    totals = lax.psum(canonical, "row")
    per_slot = jnp.sum(jnp.where(matches[:, :, None], totals[:, None, :], 0.0), axis=0)
    stored = own_cols >= 0
    per_slot = jnp.where(stored[:, None], per_slot, 1.0)
    normed = inflated * jnp.float32(rows_total) / per_slot[:, None, :]
    blended = 0.5 * flow_tiles[0].astype(jnp.float32) + 0.5 * normed
    blended = jnp.where(stored[:, None, None], blended, 0.0)
    return blended[None]


def solution(mesh):
    placed = (P("row", "col", None, None), P("row", "col"), P(("row", "col"), None))
    return jax.shard_map(
        on_device,
        mesh=mesh,
        in_specs=placed,
        out_specs=P("row", "col", None, None),
        check_vma=False,
    )
```

profile of v0, /device:TPU:0, one launch (start us, length us, event | category | flops | bytes accessed | tf_op | source)
XLA Modules:
  0.0 122.4 jit_solution(12487025733374369180)
XLA Ops:
  6.5 0.7 all-gather.4.cloned.1.call-update
  8.0 1.2 %dynamic-slice = u32[1]{0:T(128)} dynamic-slice(u32[32]{0:T(128)} %constant.69, u32[]{:T(128)S(6)} %add.57), dynamic_slice_sizes={1} | dynamic-slice | bytes 12
  9.9 0.8 bitcast_dynamic-update-slice_fusion
  10.7 8.8 %all-reduce = s32[8]{0:T(128)S(1)} all-reduce(s32[8]{0:T(128)S(1)} %bitcast_dynamic-update-slice_fusion), channel_id=1, replica_groups=mesh['row'=8,'col'=4] {'col'}, use_global_device_ids=true, to_apply=%add | all-reduce | flops 8 | bytes 64
  19.5 12.1 %all-gather = s32[8,1,2]{2,1,0:T(1,128)S(1)} all-gather(s32[1,1,2]{2,1,0:T(1,128)} %bitcast.62), channel_id=1, replica_groups=mesh['row'=8,'col'=4] {'row'}, dimensions={0}, use_global_device_ids=true | all-gather | bytes 72 | tf_op jit(solution)/shard_map/all_gather | solution.py:53
  31.7 1.3 %fusion.13 = (s32[1,1]{1,0:T(1,128)}, s32[1,1]{1,0:T(1,128)}) fusion(s32[1,2]{1,0:T(1,128)} %param.6), kind=kLoop, calls=%fused_computation.43 | loop fusion | bytes 16 | tf_op jit(solution)/shard_map/gather | solution.py:46
  32.9 1.9 %maximum_reduce_fusion = (s32[16]{0:T(128)S(1)}, s32[16]{0:T(128)S(1)}, s32[16]{0:T(128)S(1)}, s32[16]{0:T(128)S(1)}) fusion(s32[16,2]{0,1:T(2,128)} %param.7, s32[]{:T(128)} %bitcast.9, s32[]{:T(128)} %bitcast.8), kind=kLoop, calls=%fused_computation.38 | loop fusion | flops 64 | bytes 392 | tf_op jit(solution)/shard_map/max | solution.py:44
  38.5 0.7 broadcast_compare_fusion
  39.2 30.0 %all-gather.6.cloned.1.call-done = bf16[8,2,256,256]{3,2,1,0:T(8,128)(2,1)} async-done(((bf16[1,2,256,256]{3,2,1,0:T(8,128)(2,1)}), bf16[8,2,256,256]{3,2,1,0:T(8,128)(2,1)}) %all-gather.6.cloned.1.call-update) | async-done | bytes 2097168 | tf_op jit(solution)/shard_map/all_gather | solution.py:52
  69.2 29.8 %while.11 = (s32[]{:T(128)}, f32[2,256,256]{2,0,1:T(2,128)S(1)}, f32[4,4,2]{1,2,0:T(2,128)S(1)}, s32[4,4]{1,0:T(4,128)S(1)}, bf16[8,256,256]{2,1,0:T(8,128)(2,1)...) while((s32[]{:T(128)}, f32[2,256,256]{2,0,1:T(2,128)S(1)}, ...), condition=%wide.region_3.4_spmd.clone, body=%wide.region_2.3_spmd.clone.sunk | while | flops 140772416 | bytes 6296839 | solution.py:26
  69.2 1.8 %gather_fusion = bf16[4,256,256]{2,1,0:T(8,128)(2,1)S(1)} fusion(bf16[8,256,256]{2,1,0:T(8,128)(2,1)} %get-tuple-element.180, s32[1024]{0:T(1024)S(1)} %pad_clamp_fusion.3), kind=kCustom, calls=%fused_computation.clone.clone.1 | custom fusion | bytes 1048592 | tf_op jit(solution)/shard_map/while/body/eval_jaxpr/gather | solution.py:18
  71.1 2.2 %gather_fusion.1 = bf16[4,256,256]{2,1,0:T(8,128)(2,1)S(1)} fusion(bf16[8,2,256,256]{3,2,1,0:T(8,128)(2,1)} %get-tuple-element.183, s32[4]{0:T(128)S(1)} %get-tuple-element.155), kind=kCustom, calls=%fused_computation.1.clone.clone.1 | custom fusion | bytes 1048608 | tf_op jit(solution)/shard_map/while/body/eval_jaxpr/gather | solution.py:19
  73.6 3.1 %convolution_add_fusion.2 = f32[2,256,256]{2,0,1:T(2,128)S(1)} fusion(f32[4,256,256]{2,1,0:T(8,128)S(1)} %fusion.26, f32[2,256,256]{2,0,1:T(2,128)S(1)} %get-tuple-element.167, pred[]{:T(512)S(6)} %compare.10, f32[4,4,2]{1,2,0:T(2,128)S(1)} %get-tuple-element.178, s32[]{:T(128)} %get-tuple-element.166), kind=kOutput, calls=%fused_computation.3.clone.1 | convolution fusion | flops 6553600 | bytes 2098181 | tf_op jit(solution)/shard_map/while/body/eval_jaxpr/ps,pac->sac/dot_general | solution.py:23
  76.7 1.8 %gather_fusion = bf16[4,256,256]{2,1,0:T(8,128)(2,1)S(1)} fusion(bf16[8,256,256]{2,1,0:T(8,128)(2,1)} %get-tuple-element.180, s32[1024]{0:T(1024)S(1)} %pad_clamp_fusion.3), kind=kCustom, calls=%fused_computation.clone.clone.1 | custom fusion | bytes 1048592 | tf_op jit(solution)/shard_map/while/body/eval_jaxpr/gather | solution.py:18
  78.5 2.2 %gather_fusion.1 = bf16[4,256,256]{2,1,0:T(8,128)(2,1)S(1)} fusion(bf16[8,2,256,256]{3,2,1,0:T(8,128)(2,1)} %get-tuple-element.183, s32[4]{0:T(128)S(1)} %get-tuple-element.155), kind=kCustom, calls=%fused_computation.1.clone.clone.1 | custom fusion | bytes 1048608 | tf_op jit(solution)/shard_map/while/body/eval_jaxpr/gather | solution.py:19
  81.0 3.1 %convolution_add_fusion.2 = f32[2,256,256]{2,0,1:T(2,128)S(1)} fusion(f32[4,256,256]{2,1,0:T(8,128)S(1)} %fusion.26, f32[2,256,256]{2,0,1:T(2,128)S(1)} %get-tuple-element.167, pred[]{:T(512)S(6)} %compare.10, f32[4,4,2]{1,2,0:T(2,128)S(1)} %get-tuple-element.178, s32[]{:T(128)} %get-tuple-element.166), kind=kOutput, calls=%fused_computation.3.clone.1 | convolution fusion | flops 6553600 | bytes 2098181 | tf_op jit(solution)/shard_map/while/body/eval_jaxpr/ps,pac->sac/dot_general | solution.py:23
  84.2 1.8 %gather_fusion = bf16[4,256,256]{2,1,0:T(8,128)(2,1)S(1)} fusion(bf16[8,256,256]{2,1,0:T(8,128)(2,1)} %get-tuple-element.180, s32[1024]{0:T(1024)S(1)} %pad_clamp_fusion.3), kind=kCustom, calls=%fused_computation.clone.clone.1 | custom fusion | bytes 1048592 | tf_op jit(solution)/shard_map/while/body/eval_jaxpr/gather | solution.py:18
  86.0 2.2 %gather_fusion.1 = bf16[4,256,256]{2,1,0:T(8,128)(2,1)S(1)} fusion(bf16[8,2,256,256]{3,2,1,0:T(8,128)(2,1)} %get-tuple-element.183, s32[4]{0:T(128)S(1)} %get-tuple-element.155), kind=kCustom, calls=%fused_computation.1.clone.clone.1 | custom fusion | bytes 1048608 | tf_op jit(solution)/shard_map/while/body/eval_jaxpr/gather | solution.py:19
  88.5 3.1 %convolution_add_fusion.2 = f32[2,256,256]{2,0,1:T(2,128)S(1)} fusion(f32[4,256,256]{2,1,0:T(8,128)S(1)} %fusion.26, f32[2,256,256]{2,0,1:T(2,128)S(1)} %get-tuple-element.167, pred[]{:T(512)S(6)} %compare.10, f32[4,4,2]{1,2,0:T(2,128)S(1)} %get-tuple-element.178, s32[]{:T(128)} %get-tuple-element.166), kind=kOutput, calls=%fused_computation.3.clone.1 | convolution fusion | flops 6553600 | bytes 2098181 | tf_op jit(solution)/shard_map/while/body/eval_jaxpr/ps,pac->sac/dot_general | solution.py:23
  91.6 1.8 %gather_fusion = bf16[4,256,256]{2,1,0:T(8,128)(2,1)S(1)} fusion(bf16[8,256,256]{2,1,0:T(8,128)(2,1)} %get-tuple-element.180, s32[1024]{0:T(1024)S(1)} %pad_clamp_fusion.3), kind=kCustom, calls=%fused_computation.clone.clone.1 | custom fusion | bytes 1048592 | tf_op jit(solution)/shard_map/while/body/eval_jaxpr/gather | solution.py:18
  93.4 2.2 %gather_fusion.1 = bf16[4,256,256]{2,1,0:T(8,128)(2,1)S(1)} fusion(bf16[8,2,256,256]{3,2,1,0:T(8,128)(2,1)} %get-tuple-element.183, s32[4]{0:T(128)S(1)} %get-tuple-element.155), kind=kCustom, calls=%fused_computation.1.clone.clone.1 | custom fusion | bytes 1048608 | tf_op jit(solution)/shard_map/while/body/eval_jaxpr/gather | solution.py:19
  95.9 3.1 %convolution_add_fusion.2 = f32[2,256,256]{2,0,1:T(2,128)S(1)} fusion(f32[4,256,256]{2,1,0:T(8,128)S(1)} %fusion.26, f32[2,256,256]{2,0,1:T(2,128)S(1)} %get-tuple-element.167, pred[]{:T(512)S(6)} %compare.10, f32[4,4,2]{1,2,0:T(2,128)S(1)} %get-tuple-element.178, s32[]{:T(128)} %get-tuple-element.166), kind=kOutput, calls=%fused_computation.3.clone.1 | convolution fusion | flops 6553600 | bytes 2098181 | tf_op jit(solution)/shard_map/while/body/eval_jaxpr/ps,pac->sac/dot_general | solution.py:23
  99.2 15.3 %psum.7 = f32[2,256]{1,0:T(2,128)S(1)} all-reduce(f32[2,256]{1,0:T(2,128)S(1)} %select_reduce_fusion.1), channel_id=1, replica_groups=mesh['row'=8,'col'=4] {'row'}, use_global_device_ids=true, to_apply=%region_6.7 | all-reduce | flops 512 | bytes 4096 | tf_op jit(solution)/shard_map/psum | solution.py:64
  114.6 0.9 fusion.10
  (37 shorter events, 5.9 us)
Async XLA Ops:
  6.5 32.7 %all-gather.4.cloned.1.call-start = ((), (), s32[]{:S(2)}) async-start(), calls=%async_computation | async-start | bytes 1310720 | tf_op jit(solution)/shard_map/all_gather | solution.py:37
  7.3 62.0 %all-gather.6.cloned.1.call-start = ((), (), s32[]{:S(2)}) async-start(), calls=%async_computation.1 | async-start | bytes 2359296 | tf_op jit(solution)/shard_map/all_gather | solution.py:52
  69.2 45.4 %copy-start = (bf16[1,2,256,256]{3,2,1,0:T(8,128)(2,1)S(1)}, bf16[1,2,256,256]{3,2,1,0:T(8,128)(2,1)}, u32[]{:S(2)}) copy-start(bf16[1,2,256,256]{3,2,1,0:T(8,128)(2,1)} %param.5) | copy-start | bytes 786436
Sparse Core Ops, SparseCore 0:
  9.2 29.2 all-gather.3
  40.0 29.1 all-gather.5
where the time goes:
time: 123 us; the launch traced here: 122 us
  blocking collectives  36.2 us (29%)
  waiting for transfers between devices  31.4 us (26%)
  local copies, waits for them, and re-layouts  20.2 us (16%)
  between operations  14.1 us (11%)
  matrix products  13.6 us (11%)
  other arithmetic  6.59 us (5%)
    all_gather x1, waiting for transfers between devices, on_device(): lax.all_gather(flow_tiles, 'row', axis=0, tiled=True)  30 us
    psum x1, blocking collectives, on_device(): totals = lax.psum(canonical, 'row')  15.3 us
    dot_general x4, matrix products, block_step(): jnp.einsum('ps,pac->sac', weight_block, products, precision=lax.Precision...  12.4 us
    all_gather x1, blocking collectives, on_device(): lax.all_gather(tile_cols, 'row', axis=0, tiled=True)  12.1 us
    unnamed x1, blocking collectives  8.85 us
    gather x4, local copies, waits for them, and re-layouts, block_step(): right_tiles = right_source[row_pick, slot_pick]  8.69 us
    gather x4, local copies, waits for them, and re-layouts, block_step(): left_tiles = left_source[left_pick]  7.26 us
  transfers between devices with their start and end apart: 2, of which 1 were waited for; matrix products, arithmetic and copies ran while one was open for 8% of the time, Pallas kernels for 0%

commit v1 on v0

v1 whole, which is shorter than its diff:
```python
import functools
import math

import jax
import jax.numpy as jnp
from jax import lax
from jax.experimental import pallas as pl
from jax.experimental.pallas import tpu as pltpu
from jax.sharding import PartitionSpec as P

MESH = pl.DeviceIdType.MESH
CORES = 2
SPLIT = 2


def remote(src, dst, send_sem, recv_sem, device):
    return pltpu.make_async_remote_copy(
        src_ref=src,
        dst_ref=dst,
        send_sem=send_sem,
        recv_sem=recv_sem,
        device_id=device,
        device_id_type=MESH,
    )


def kernel(
    nrow, ncol, cols_ref, flow_ref, out_ref,
    own, blocks, left, acc, sums,
    up_send, dn_send, mate_send, recv, col_send, col_recv, sum_send, sum_recv,
):
    tiles, width = flow_ref.shape[1], flow_ref.shape[3]
    chunks, depth = own.shape[0], own.shape[1]
    planes = nrow // CORES
    row, col = lax.axis_index("row"), lax.axis_index("col")
    z, core = row // CORES, row % CORES
    mate = (row + 1 - 2 * core, col)
    above, below = (row + CORES, col), (row - CORES, col)
    has_above, has_below = z < planes - 1, z > 0
    ny = math.isqrt(ncol)
    ny = ny if ny * ny == ncol else 1
    nx = ncol // ny
    y, x = col // nx, col % nx
    peers = []
    for dy in range(ny):
        for dx in range(nx):
            if dy or dx:
                peers.append((dy * nx + dx, ((y + dy) % ny) * nx + (x + dx) % nx))
    peers.sort(key=lambda p: (p[0] // nx > 0) + (p[0] % nx > 0))

    barrier = pltpu.get_barrier_semaphore()

    def greet(device):
        pl.semaphore_signal(barrier, inc=1, device_id=device, device_id_type=MESH)

    greet(mate)
    for _, peer in peers:
        greet((row, peer))

    @pl.when(has_above)
    def _():
        greet(above)

    @pl.when(has_below)
    def _():
        greet(below)

    kept = []
    for t in range(tiles):
        target = col + ncol * t
        tile = jnp.zeros((width, width), jnp.float32)
        weight = jnp.float32(0)
        for s in range(tiles):
            w = (cols_ref[0, s] == target).astype(jnp.float32)
            weight = weight + w
            tile = tile + flow_ref[0, s].astype(jnp.float32) * w
        kept.append(weight)
        tile = tile.astype(jnp.bfloat16)
        own[t * SPLIT:(t + 1) * SPLIT] = tile.reshape(SPLIT, depth, width)
        left[col, t] = tile
    blocks[row] = own[...]

    ends = jnp.where(has_above, 1, 0) + jnp.where(has_below, 1, 0)
    pl.semaphore_wait(barrier, ncol + ends)

    def to_above(step, k, q, src):
        return remote(src, blocks.at[k, q], up_send.at[step, q], recv.at[k, q], above)

    def to_below(step, k, q, src):
        return remote(src, blocks.at[k, q], dn_send.at[step, q], recv.at[k, q], below)

    def to_mate(plane, k, q, src):
        return remote(src, blocks.at[k, q], mate_send.at[plane, q], recv.at[k, q], mate)

    def arrived(k, q):
        remote(own.at[q], blocks.at[k, q], mate_send.at[0, q], recv.at[k, q], mate).wait_recv()

    def to_peer(slot, peer):
        return remote(
            blocks_as_tiles(), left.at[col], col_send.at[slot], col_recv.at[col], (row, peer)
        )

    def blocks_as_tiles():
        return left.at[col]

    for q in range(chunks):

        @pl.when(has_above)
        def _():
            to_above(0, row, q, own.at[q]).start()

        @pl.when(has_below)
        def _():
            to_below(0, row, q, own.at[q]).start()

        if q == 0:
            for slot, peer in peers:
                to_peer(slot, peer).start()
        to_mate(z, row, q, own.at[q]).start()

    acc[...] = jnp.zeros_like(acc)

    def relay(step, q):
        @pl.when(z >= step)
        def _():
            k = row - CORES * step
            arrived(k, q)

            @pl.when(has_above)
            def _():
                to_above(step, k, q, blocks.at[k, q]).start()

            to_mate(z - step, k, q, blocks.at[k, q]).start()

        @pl.when(z + step < planes)
        def _():
            k = row + CORES * step
            arrived(k, q)

            @pl.when(has_below)
            def _():
                to_below(step, k, q, blocks.at[k, q]).start()

            to_mate(z + step, k, q, blocks.at[k, q]).start()

    def multiply(k):
        a = left[k % ncol, k // ncol]
        for t in range(tiles):
            b = blocks[k, pl.ds(t * SPLIT, SPLIT)].reshape(width, width)
            acc[t] += jnp.dot(a, b, preferred_element_type=jnp.float32)

    def multiply_chunk(k, q):
        part = pl.ds((q % SPLIT) * depth, depth)
        a = left[k % ncol, k // ncol, :, part]
        acc[q // SPLIT] += jnp.dot(a, blocks[k, q], preferred_element_type=jnp.float32)

    def compute(distance):
        for sign in (-1, 1) if distance else (1,):
            plane = z + sign * distance

            @pl.when((plane >= 0) & (plane < planes))
            def _():
                mine = plane * CORES + core
                multiply(mine)
                other = plane * CORES + 1 - core
                for q in range(chunks):
                    arrived(other, q)
                multiply(other)

    def last(distance):
        for sign in (-1, 1):
            plane = z + sign * distance

            @pl.when((plane >= 0) & (plane < planes))
            def _():
                mine = plane * CORES + core
                other = plane * CORES + 1 - core
                for q in range(chunks):
                    arrived(mine, q)
                    to_mate(plane, mine, q, blocks.at[mine, q]).start()
                    multiply_chunk(mine, q)
                    if q:
                        arrived(other, q - 1)
                        multiply_chunk(other, q - 1)
                arrived(other, chunks - 1)
                multiply_chunk(other, chunks - 1)

    done = 0

    def catch_up(upto):
        nonlocal done
        if done == 0:
            for slot, peer in peers:
                remote(
                    left.at[peer], left.at[peer], col_send.at[slot], col_recv.at[peer], (row, peer)
                ).wait_recv()
        while done < upto:
            compute(done)
            done += 1

    for step in range(1, planes - 1):
        if step > 2:
            catch_up(step)
        for q in range(chunks):
            relay(step, q)
    catch_up(planes - 1)
    last(planes - 1)

    for t in range(tiles):
        squares = acc[t] * acc[t]
        acc[t] = squares
        sums[row, t] = jnp.sum(squares, axis=0) * kept[t]

    def to_row(d):
        other = (row + d) % nrow
        return other, remote(
            sums.at[row], sums.at[row], sum_send.at[d], sum_recv.at[row], (other, col)
        )

    for d in range(1, nrow):
        to_row(d)[1].start()
    for d in range(1, nrow):
        other, _ = to_row(d)
        remote(
            sums.at[other], sums.at[other], sum_send.at[d], sum_recv.at[other], (other, col)
        ).wait_recv()
    totals = sums[0]
    for k in range(1, nrow):
        totals = totals + sums[k]
    for s in range(tiles):
        out = jnp.zeros((width, width), jnp.float32)
        held = jnp.float32(0)
        for t in range(tiles):
            w = (cols_ref[0, s] == col + ncol * t).astype(jnp.float32)
            held = held + w
            safe = jnp.where(totals[t] > 0, totals[t], 1.0)
            scale = jnp.float32(0.5 * nrow * width) / safe * w
            out = out + acc[t] * scale[None, :]
        out_ref[0, s] = out + flow_ref[0, s].astype(jnp.float32) * (0.5 * held)

    for q in range(chunks):
        for step in range(planes):
            @pl.when(has_above & (z >= step))
            def _():
                to_above(step, row, q, own.at[q]).wait_send()

            @pl.when(has_below & (z + step < planes))
            def _():
                to_below(step, row, q, own.at[q]).wait_send()

            to_mate(step, row, q, own.at[q]).wait_send()
    for slot, peer in peers:
        to_peer(slot, peer).wait_send()
    for d in range(1, nrow):
        to_row(d)[1].wait_send()


def on_device(nrow, ncol, flow_tiles, tile_cols, pairs):
    _, tiles, _, width = flow_tiles.shape
    planes, chunks, depth = nrow // CORES, tiles * SPLIT, width // SPLIT
    dma = pltpu.SemaphoreType.DMA
    return pl.pallas_call(
        functools.partial(kernel, nrow, ncol),
        out_shape=jax.ShapeDtypeStruct(flow_tiles.shape, jnp.float32),
        in_specs=[
            pl.BlockSpec(memory_space=pltpu.SMEM),
            pl.BlockSpec(memory_space=pltpu.VMEM),
        ],
        out_specs=pl.BlockSpec(memory_space=pltpu.VMEM),
        scratch_shapes=[
            pltpu.VMEM((chunks, depth, width), jnp.bfloat16),
            pltpu.VMEM((nrow, chunks, depth, width), jnp.bfloat16),
            pltpu.VMEM((ncol, tiles, width, width), jnp.bfloat16),
            pltpu.VMEM((tiles, width, width), jnp.float32),
            pltpu.VMEM((nrow, tiles, width), jnp.float32),
            dma((planes, chunks)),
            dma((planes, chunks)),
            dma((planes, chunks)),
            dma((nrow, chunks)),
            dma((ncol,)),
            dma((ncol,)),
            dma((nrow,)),
            dma((nrow,)),
        ],
        compiler_params=pltpu.CompilerParams(
            collective_id=0, has_side_effects=True, vmem_limit_bytes=48 * 1024 * 1024
        ),
        name="cluster_step",
    )(tile_cols, flow_tiles)


def solution(mesh):
    placed = (P("row", "col", None, None), P("row", "col"), P(("row", "col"), None))
    return jax.shard_map(
        functools.partial(on_device, mesh.shape["row"], mesh.shape["col"]),
        mesh=mesh,
        in_specs=placed,
        out_specs=P("row", "col", None, None),
        check_vma=False,
    )
```

time: 123 us -> 32 us (0.26)
  blocking collectives: 36.2 us -> 0 us
  waiting for transfers between devices: 31.4 us -> 0 us
  Pallas kernels: 0 us -> 29.5 us
  local copies, waits for them, and re-layouts: 20.2 us -> 2.4 us
  between operations: 14.1 us -> 0.01 us
  matrix products: 13.6 us -> 0 us
  other arithmetic: 6.59 us -> 0 us
    all_gather x2 -> x0, waiting for transfers between devices: 30 us -> none  [the longest x1 30 us: on_device(): lax.all_gather(flow_tiles, 'row', axis=0, tiled=True)]
    pallas_call x0 -> x1, Pallas kernels: none -> 29.5 us  [on_device(): pl.pallas_call(functools.partial(kernel, nrow, ncol), out_shape=jax.Shape...]
    gather x10 -> x0, local copies, waits for them, and re-layouts: 17.8 us -> none  [the longest x4 8.69 us: block_step(): right_tiles = right_source[row_pick, slot_pick]]
    psum x1 -> x0, blocking collectives: 15.3 us -> none  [on_device(): totals = lax.psum(canonical, 'row')]
    dot_general x8 -> x0, matrix products: 13.6 us -> none  [the longest x4 12.4 us: block_step(): jnp.einsum('ps,pac->sac', weight_block, products, precision=lax.Precision...]
    all_gather x1 -> x0, blocking collectives: 12.1 us -> none  [on_device(): lax.all_gather(tile_cols, 'row', axis=0, tiled=True)]
    unnamed x1 -> x0, blocking collectives: 8.85 us -> none
    max x1 -> x0, other arithmetic: 1.93 us -> none  [on_device(): inner_safe = jnp.maximum(inner_tile, 0)]
  transfers between devices with their start and end apart: 2 -> 0, of which waited for: 1 -> 0; matrix products, arithmetic and copies ran while one was open for 8% -> 0% of each run, Pallas kernels for 0% -> 0%
where the time goes in v1:
time: 32 us; the launch traced here: 31.9 us
  Pallas kernels  29.5 us (92%)
  local copies, waits for them, and re-layouts  2.4 us (8%)
    pallas_call x1, Pallas kernels, on_device(): pl.pallas_call(functools.partial(kernel, nrow, ncol), out_shape=jax.Shape...  29.5 us
    unnamed x5, local copies, waits for them, and re-layouts  2.4 us

profile of v1, /device:TPU:0, one launch (start us, length us, event | category | flops | bytes accessed | tf_op | source)
XLA Modules:
  0.0 31.9 jit_solution(845247389002245544)
XLA Ops:
  0.0 0.0 copy-start
  0.0 0.9 %copy-done = bf16[1,2,256,256]{3,2,1,0:T(8,128)(2,1)S(1)} copy-done((bf16[1,2,256,256]{3,2,1,0:T(8,128)(2,1)S(1)}, bf16[1,2,256,256]{3,2,1,0:T(8,128)(2,1)}, u32[]{:S(2)}) %copy-start) | copy-done | bytes 262168
  1.0 0.0 copy-start.1
  1.0 0.7 %copy-done.1 = s32[1,2]{1,0:T(1,128)S(1)} copy-done((s32[1,2]{1,0:T(1,128)S(1)}, s32[1,2]{1,0:T(1,128)}, u32[]{:S(2)}) %copy-start.1) | copy-done | bytes 32
  1.6 29.5 %cluster_step.1 = f32[1,2,256,256]{3,2,1,0:T(8,128)S(1)} custom-call(s32[1,2]{1,0:T(1,128)S(1)} %copy-done.1, bf16[1,2,256,256]{3,2,1,0:T(8,128)(2,1)S(1)} %copy-done), custom_call_target="tpu_custom_call" | custom-call | tf_op jit(solution)/shard_map/cluster_step/pallas_call | solution.py:262
  31.1 0.8 %copy.4 = f32[1,2,256,256]{3,2,1,0:T(8,128)} copy(f32[1,2,256,256]{3,2,1,0:T(8,128)S(1)} %cluster_step.1) | data formatting | bytes 1048576
Async XLA Ops:
  0.0 0.9 %copy-start = (bf16[1,2,256,256]{3,2,1,0:T(8,128)(2,1)S(1)}, bf16[1,2,256,256]{3,2,1,0:T(8,128)(2,1)}, u32[]{:S(2)}) copy-start(bf16[1,2,256,256]{3,2,1,0:T(8,128)(2,1)} %flow_ref.1) | copy-start | bytes 786436
  1.0 0.7 %copy-start.1 = (s32[1,2]{1,0:T(1,128)S(1)}, s32[1,2]{1,0:T(1,128)}, u32[]{:S(2)}) copy-start(s32[1,2]{1,0:T(1,128)} %cols_ref.1) | copy-start | bytes 28

commit v2 on v1

v2 whole, which is shorter than its diff:
```python
import functools
import math

import jax
import jax.numpy as jnp
from jax import lax
from jax.experimental import pallas as pl
from jax.experimental.pallas import tpu as pltpu
from jax.sharding import PartitionSpec as P

MESH = pl.DeviceIdType.MESH
CORES = 2
SPLIT = 2


def remote(src, dst, send_sem, recv_sem, device):
    return pltpu.make_async_remote_copy(
        src_ref=src,
        dst_ref=dst,
        send_sem=send_sem,
        recv_sem=recv_sem,
        device_id=device,
        device_id_type=MESH,
    )


def kernel(
    nrow, ncol, cols_hbm, flow_hbm, out_ref,
    cols, raw, own, blocks, left, acc, swap, result, flags, sums,
    in_sem, up_send, dn_send, mate_send, recv, left_send, left_recv,
    left_mate, flag_sem, swap_sem, sum_send, sum_recv,
):
    tiles, width = raw.shape[0], raw.shape[2]
    depth = own.shape[1]
    share = tiles // CORES
    pieces = share * SPLIT
    planes = nrow // CORES
    row, col = lax.axis_index("row"), lax.axis_index("col")
    z, core = row // CORES, row % CORES
    mate = (row + 1 - 2 * core, col)
    mate_row = row + 1 - 2 * core
    above, below = (row + CORES, col), (row - CORES, col)
    has_above, has_below = z < planes - 1, z > 0
    ny = math.isqrt(ncol)
    ny = ny if ny * ny == ncol else 1
    nx = ncol // ny
    y, x = col // nx, col % nx
    peers = []
    for dy in range(ny):
        for dx in range(nx):
            if dy or dx:
                peers.append((dy * nx + dx, ((y + dy) % ny) * nx + (x + dx) % nx))
    peers.sort(key=lambda p: (p[0] // nx > 0) + (p[0] % nx > 0))

    load_cols = pltpu.make_async_copy(cols_hbm, cols, in_sem.at[0])
    load_flow = pltpu.make_async_copy(flow_hbm.at[0], raw, in_sem.at[1])
    load_cols.start()
    load_flow.start()

    barrier = pltpu.get_barrier_semaphore()

    def greet(device):
        pl.semaphore_signal(barrier, inc=1, device_id=device, device_id_type=MESH)

    greet(mate)
    for _, peer in peers:
        greet((row, peer))

    @pl.when(has_above)
    def _():
        for c in range(CORES):
            greet(((z + 1) * CORES + c, col))

    @pl.when(has_below)
    def _():
        for c in range(CORES):
            greet(((z - 1) * CORES + c, col))

    load_cols.wait()
    load_flow.wait()
    for t in range(tiles):
        target = col + ncol * t
        tile = jnp.zeros((width, width), jnp.float32)
        weight = jnp.float32(0)
        for s in range(tiles):
            w = (cols[0, s] == target).astype(jnp.float32)
            weight = weight + w
            tile = tile + raw[s].astype(jnp.float32) * w
        flags[core, t] = jnp.full((width,), weight, jnp.float32)
        tile = tile.astype(jnp.bfloat16)
        own[t * SPLIT:(t + 1) * SPLIT] = tile.reshape(SPLIT, depth, width)
        left[col, t, core] = tile
    blocks[row] = own[pl.ds(core * pieces, pieces)]

    ends = jnp.where(has_above, 1, 0) + jnp.where(has_below, 1, 0)
    pl.semaphore_wait(barrier, ncol + CORES * ends)

    def piece(src, k, u, send_sem, device):
        return remote(src, blocks.at[k, u], send_sem, recv.at[k, u], device)

    def arrived(k, u):
        piece(own.at[u], k, u, mate_send.at[u], mate).wait_recv()

    def to_mate(u):
        return piece(own.at[(1 - core) * pieces + u], row, u, mate_send.at[u], mate)

    def left_copy(slot, c, rc, device, send_sem):
        part = left.at[c, :, rc]
        return remote(part, part, send_sem, left_recv.at[rc, c], device)

    flag_copy = remote(flags.at[core], flags.at[core], flag_sem.at[0], flag_sem.at[1], mate)

    for u in range(pieces):
        for c in range(CORES):

            @pl.when(has_above)
            def _():
                piece(
                    own.at[c * pieces + u], row, u, up_send.at[0, c * pieces + u],
                    ((z + 1) * CORES + c, col),
                ).start()

            @pl.when(has_below)
            def _():
                piece(
                    own.at[c * pieces + u], row, u, dn_send.at[0, c * pieces + u],
                    ((z - 1) * CORES + c, col),
                ).start()

        if u == 0:
            for slot, peer in peers:
                left_copy(slot, col, core, (row, peer), left_send.at[slot]).start()
    for u in range(pieces):
        to_mate(u).start()
    left_copy(0, col, core, mate, left_mate.at[col]).start()
    flag_copy.start()

    acc[...] = jnp.zeros_like(acc)

    def relay(step):
        for c in range(CORES):
            for u in range(pieces):

                @pl.when(z >= step)
                def _():
                    k = (z - step) * CORES + c
                    arrived(k, u)

                    @pl.when(has_above)
                    def _():
                        piece(
                            blocks.at[k, u], k, u, up_send.at[step, c * pieces + u], above
                        ).start()

                @pl.when(z + step < planes)
                def _():
                    k = (z + step) * CORES + c
                    arrived(k, u)

                    @pl.when(has_below)
                    def _():
                        piece(
                            blocks.at[k, u], k, u, dn_send.at[step, c * pieces + u], below
                        ).start()

    def multiply(k):
        a = left[k % ncol, k // ncol].reshape(CORES * width, width)
        for i in range(share):
            b = blocks[k, pl.ds(i * SPLIT, SPLIT)].reshape(width, width)
            c = jnp.dot(a, b, preferred_element_type=jnp.float32)
            acc[i] += c.reshape(CORES, width, width)

    def multiply_piece(k, u):
        h = u % SPLIT
        a = left[k % ncol, k // ncol, :, :, pl.ds(h * depth, depth)]
        c = jnp.dot(
            a.reshape(CORES * width, depth), blocks[k, u], preferred_element_type=jnp.float32
        )
        acc[u // SPLIT] += c.reshape(CORES, width, width)

    def compute(distance):
        for sign in (-1, 1) if distance else (1,):
            plane = z + sign * distance

            @pl.when((plane >= 0) & (plane < planes))
            def _():
                if distance == 0:
                    for u in range(pieces):
                        arrived(mate_row, u)
                for c in range(CORES):
                    multiply(plane * CORES + c)

    def last(distance):
        for sign in (-1, 1):
            plane = z + sign * distance

            @pl.when((plane >= 0) & (plane < planes))
            def _():
                for c in range(CORES):
                    for u in range(pieces):
                        k = plane * CORES + c
                        arrived(k, u)
                        multiply_piece(k, u)

    done = 0

    def catch_up(upto):
        nonlocal done
        if done == 0:
            for slot, peer in peers:
                left_copy(slot, peer, core, mate, left_mate.at[peer]).wait_recv()
                left_copy(slot, peer, core, mate, left_mate.at[peer]).start()
            for c in range(ncol):
                left_copy(0, c, 1 - core, mate, left_mate.at[c]).wait_recv()
        while done < upto:
            compute(done)
            done += 1

    for step in range(1, planes - 1):
        if step > 2:
            catch_up(step)
        relay(step)
    catch_up(planes - 1)
    last(planes - 1)
    flag_copy.wait_recv()

    for i in range(share):
        t = core * share + i
        part = jnp.zeros((width,), jnp.float32)
        for c in range(CORES):
            part = part + jnp.sum(acc[i, c] * acc[i, c], axis=0) * flags[c, t]
        sums[row, i] = part

    def to_row(d):
        return remote(
            sums.at[row], sums.at[row], sum_send.at[d], sum_recv.at[row],
            ((row + d) % nrow, col),
        )

    for d in range(1, nrow):
        to_row(d).start()

    for i in range(share):
        other = acc[i, 1 - core]
        swap[i] = other * other
    swap_copy = remote(
        swap, result.at[pl.ds(core * share, share)], swap_sem.at[0], swap_sem.at[1], mate
    )
    swap_copy.start()
    for i in range(share):
        mine = acc[i, core]
        result[core * share + i] = mine * mine
    swap_copy.wait_recv()

    for d in range(1, nrow):
        other = (row + d) % nrow
        remote(
            sums.at[other], sums.at[other], sum_send.at[d], sum_recv.at[other], (other, col)
        ).wait_recv()
    for s in range(tiles):
        out = jnp.zeros((width, width), jnp.float32)
        held = jnp.float32(0)
        for t in range(tiles):
            w = (cols[0, s] == col + ncol * t).astype(jnp.float32)
            held = held + w
            total = sums[t // share, t % share]
            for p in range(1, planes):
                total = total + sums[p * CORES + t // share, t % share]
            safe = jnp.where(total > 0, total, 1.0)
            scale = jnp.float32(0.5 * nrow * width) / safe * w
            out = out + result[t] * scale[None, :]
        out_ref[0, s] = out + raw[s].astype(jnp.float32) * (0.5 * held)
    for n in range(CORES * pieces):
        for step in range(planes):

            @pl.when(has_above & (z >= step))
            def _():
                piece(own.at[n], row, 0, up_send.at[step, n], above).wait_send()

            @pl.when(has_below & (z + step < planes))
            def _():
                piece(own.at[n], row, 0, dn_send.at[step, n], below).wait_send()

    for u in range(pieces):
        to_mate(u).wait_send()
    for slot, peer in peers:
        left_copy(slot, col, core, (row, peer), left_send.at[slot]).wait_send()
    for c in range(ncol):
        left_copy(0, c, core, mate, left_mate.at[c]).wait_send()
    flag_copy.wait_send()
    swap_copy.wait_send()
    for d in range(1, nrow):
        to_row(d).wait_send()


def on_device(nrow, ncol, flow_tiles, tile_cols, pairs):
    _, tiles, _, width = flow_tiles.shape
    planes, depth, share = nrow // CORES, width // SPLIT, tiles // CORES
    pieces = share * SPLIT
    dma = pltpu.SemaphoreType.DMA
    return pl.pallas_call(
        functools.partial(kernel, nrow, ncol),
        out_shape=jax.ShapeDtypeStruct(flow_tiles.shape, jnp.float32),
        in_specs=[pl.BlockSpec(memory_space=pl.ANY), pl.BlockSpec(memory_space=pl.ANY)],
        out_specs=pl.BlockSpec(memory_space=pltpu.VMEM),
        scratch_shapes=[
            pltpu.SMEM((1, tiles), jnp.int32),
            pltpu.VMEM((tiles, width, width), jnp.bfloat16),
            pltpu.VMEM((CORES * pieces, depth, width), jnp.bfloat16),
            pltpu.VMEM((nrow, pieces, depth, width), jnp.bfloat16),
            pltpu.VMEM((ncol, tiles, CORES, width, width), jnp.bfloat16),
            pltpu.VMEM((share, CORES, width, width), jnp.float32),
            pltpu.VMEM((share, width, width), jnp.float32),
            pltpu.VMEM((tiles, width, width), jnp.float32),
            pltpu.VMEM((CORES, tiles, width), jnp.float32),
            pltpu.VMEM((nrow, share, width), jnp.float32),
            dma((2,)),
            dma((planes, CORES * pieces)),
            dma((planes, CORES * pieces)),
            dma((pieces,)),
            dma((nrow, pieces)),
            dma((ncol,)),
            dma((CORES, ncol)),
            dma((ncol,)),
            dma((2,)),
            dma((2,)),
            dma((nrow,)),
            dma((nrow,)),
        ],
        compiler_params=pltpu.CompilerParams(
            collective_id=0, has_side_effects=True, vmem_limit_bytes=60 * 1024 * 1024
        ),
        name="cluster_step",
    )(tile_cols, flow_tiles)


def solution(mesh):
    placed = (P("row", "col", None, None), P("row", "col"), P(("row", "col"), None))
    return jax.shard_map(
        functools.partial(on_device, mesh.shape["row"], mesh.shape["col"]),
        mesh=mesh,
        in_specs=placed,
        out_specs=P("row", "col", None, None),
        check_vma=False,
    )
```

time: 32 us -> 30.6 us (0.956)
  Pallas kernels: 29.5 us -> 28.6 us
  local copies, waits for them, and re-layouts: 2.4 us -> 1.87 us
    pallas_call x1, Pallas kernels: 29.5 us -> 28.6 us  [on_device(): pl.pallas_call(functools.partial(kernel, nrow, ncol), out_shape=jax.Shape...]
    unnamed x5 -> x1, local copies, waits for them, and re-layouts: 2.4 us -> 1.87 us
where the time goes in v2:
time: 30.6 us; the launch traced here: 30.5 us
  Pallas kernels  28.6 us (93%)
  local copies, waits for them, and re-layouts  1.87 us (6%)
    pallas_call x1, Pallas kernels, on_device(): pl.pallas_call(functools.partial(kernel, nrow, ncol), out_shape=jax.Shape...  28.6 us
    unnamed x1, local copies, waits for them, and re-layouts  1.87 us

profile of v2, /device:TPU:0, one launch (start us, length us, event | category | flops | bytes accessed | tf_op | source)
XLA Modules:
  0.0 30.5 jit_solution(664011496642117351)
XLA Ops:
  0.0 28.6 %cluster_step.1 = f32[1,2,256,256]{3,2,1,0:T(8,128)} custom-call(s32[1,2]{1,0:T(1,128)} %cols_hbm.1, bf16[1,2,256,256]{3,2,1,0:T(8,128)(2,1)} %flow_hbm.1), custom_call_target="tpu_custom_call" | custom-call | tf_op jit(solution)/shard_map/cluster_step/pallas_call | solution.py:301
  28.6 1.9 %copy.4 = f32[1,2,256,256]{3,2,1,0:T(8,128)} copy(f32[1,2,256,256]{3,2,1,0:T(8,128)} %cluster_step.1) | data formatting | bytes 1048576

commit v3 on v2

--- a/solution.py
+++ b/solution.py
@@ -25,9 +25,9 @@
 
 
 def kernel(
-    nrow, ncol, cols_hbm, flow_hbm, out_ref,
-    cols, raw, own, blocks, left, acc, swap, result, flags, sums,
-    in_sem, up_send, dn_send, mate_send, recv, left_send, left_recv,
+    nrow, ncol, cols_hbm, flow_hbm, squares_ref, scale_ref,
+    cols, raw, own, blocks, left, acc, swap, result, placed, flags, sums,
+    in_sem, out_sem, up_send, dn_send, mate_send, recv, left_send, left_recv,
     left_mate, flag_sem, swap_sem, sum_send, sum_recv,
 ):
     tiles, width = raw.shape[0], raw.shape[2]
@@ -45,12 +45,14 @@
     ny = ny if ny * ny == ncol else 1
     nx = ncol // ny
     y, x = col // nx, col % nx
-    peers = []
-    for dy in range(ny):
-        for dx in range(nx):
-            if dy or dx:
-                peers.append((dy * nx + dx, ((y + dy) % ny) * nx + (x + dx) % nx))
-    peers.sort(key=lambda p: (p[0] // nx > 0) + (p[0] % nx > 0))
+    half = tiles // 2
+
+    def at(dy, dx):
+        return ((y + dy) % ny) * nx + (x + dx) % nx
+
+    along_x = [(0, dx) for dx in range(1, nx)]
+    along_y = [(dy, 0) for dy in range(1, ny)]
+    across = [(dy, dx) for dy, _ in along_y for _, dx in along_x]
 
     load_cols = pltpu.make_async_copy(cols_hbm, cols, in_sem.at[0])
     load_flow = pltpu.make_async_copy(flow_hbm.at[0], raw, in_sem.at[1])
@@ -63,8 +65,8 @@
         pl.semaphore_signal(barrier, inc=1, device_id=device, device_id_type=MESH)
 
     greet(mate)
-    for _, peer in peers:
-        greet((row, peer))
+    for d in along_x + along_y:
+        greet((row, at(*d)))
 
     @pl.when(has_above)
     def _():
@@ -93,7 +95,7 @@
     blocks[row] = own[pl.ds(core * pieces, pieces)]
 
     ends = jnp.where(has_above, 1, 0) + jnp.where(has_below, 1, 0)
-    pl.semaphore_wait(barrier, ncol + CORES * ends)
+    pl.semaphore_wait(barrier, nx + ny - 1 + CORES * ends)
 
     def piece(src, k, u, send_sem, device):
         return remote(src, blocks.at[k, u], send_sem, recv.at[k, u], device)
@@ -104,9 +106,33 @@
     def to_mate(u):
         return piece(own.at[(1 - core) * pieces + u], row, u, mate_send.at[u], mate)
 
-    def left_copy(slot, c, rc, device, send_sem):
-        part = left.at[c, :, rc]
-        return remote(part, part, send_sem, left_recv.at[rc, c], device)
+    def left_copy(c, t, rc, device, send_sem):
+        part = left.at[c, t, rc]
+        return remote(part, part, send_sem, left_recv.at[rc, c, t], device)
+
+    def left_out(source, move, t):
+        slot = (source[0] + move[0]) * nx + source[1] + move[1]
+        return left_copy(at(*source), t, core, (row, at(*move)), left_send.at[slot, t])
+
+    def left_to_mate(source, t):
+        c = at(*source)
+        return left_copy(c, t, core, mate, left_mate.at[c, t])
+
+    def left_arrived(source, t):
+        left_to_mate(source, t).wait_recv()
+        left_to_mate(source, t).start()
+
+    def left_relay():
+        for t in range(half):
+            for d in along_x:
+                left_arrived(d, t)
+                for move in along_y:
+                    left_out(d, move, t).start()
+        for t in range(half, tiles):
+            for d in along_y:
+                left_arrived(d, t)
+                for move in along_x:
+                    left_out(d, move, t).start()
 
     flag_copy = remote(flags.at[core], flags.at[core], flag_sem.at[0], flag_sem.at[1], mate)
 
@@ -128,17 +154,23 @@
                 ).start()
 
         if u == 0:
-            for slot, peer in peers:
-                left_copy(slot, col, core, (row, peer), left_send.at[slot]).start()
+            for t in range(tiles):
+                for d in along_x:
+                    left_out((0, 0), d, t).start()
+                for d in along_y:
+                    left_out((0, 0), d, tiles - 1 - t).start()
     for u in range(pieces):
         to_mate(u).start()
-    left_copy(0, col, core, mate, left_mate.at[col]).start()
+    for t in range(tiles):
+        left_to_mate((0, 0), t).start()
     flag_copy.start()
 
     acc[...] = jnp.zeros_like(acc)
 
     def relay(step):
         for c in range(CORES):
+            if step == 1 and c == CORES - 1:
+                left_relay()
             for u in range(pieces):
 
                 @pl.when(z >= step)
@@ -207,11 +239,12 @@
     def catch_up(upto):
         nonlocal done
         if done == 0:
-            for slot, peer in peers:
-                left_copy(slot, peer, core, mate, left_mate.at[peer]).wait_recv()
-                left_copy(slot, peer, core, mate, left_mate.at[peer]).start()
+            for d in across:
+                for t in range(tiles):
+                    left_arrived(d, t)
             for c in range(ncol):
-                left_copy(0, c, 1 - core, mate, left_mate.at[c]).wait_recv()
+                for t in range(tiles):
+                    left_copy(c, t, 1 - core, mate, left_mate.at[c, t]).wait_recv()
         while done < upto:
             compute(done)
             done += 1
@@ -220,6 +253,13 @@
         if step > 2:
             catch_up(step)
         relay(step)
+        if step == 1:
+            for t in range(half, tiles):
+                for d in along_x:
+                    left_arrived(d, t)
+            for t in range(half):
+                for d in along_y:
+                    left_arrived(d, t)
     catch_up(planes - 1)
     last(planes - 1)
     flag_copy.wait_recv()
@@ -252,24 +292,37 @@
         result[core * share + i] = mine * mine
     swap_copy.wait_recv()
 
+    weights = [
+        [(cols[0, s] == col + ncol * t).astype(jnp.float32) for t in range(tiles)]
+        for s in range(tiles)
+    ]
+    for s in range(tiles):
+        chosen = jnp.zeros((width, width), jnp.float32)
+        for t in range(tiles):
+            chosen = chosen + result[t] * weights[s][t]
+        placed[s] = chosen
+    store = pltpu.make_async_copy(placed, squares_ref.at[0], out_sem)
+    store.start()
+
     for d in range(1, nrow):
         other = (row + d) % nrow
         remote(
             sums.at[other], sums.at[other], sum_send.at[d], sum_recv.at[other], (other, col)
         ).wait_recv()
+    scales = []
+    for t in range(tiles):
+        total = sums[t // share, t % share]
+        for p in range(1, planes):
+            total = total + sums[p * CORES + t // share, t % share]
+        safe = jnp.where(total > 0, total, 1.0)
+        scales.append(jnp.float32(0.5 * nrow * width) / safe)
     for s in range(tiles):
-        out = jnp.zeros((width, width), jnp.float32)
-        held = jnp.float32(0)
+        scale = jnp.zeros((width,), jnp.float32)
         for t in range(tiles):
-            w = (cols[0, s] == col + ncol * t).astype(jnp.float32)
-            held = held + w
-            total = sums[t // share, t % share]
-            for p in range(1, planes):
-                total = total + sums[p * CORES + t // share, t % share]
-            safe = jnp.where(total > 0, total, 1.0)
-            scale = jnp.float32(0.5 * nrow * width) / safe * w
-            out = out + result[t] * scale[None, :]
-        out_ref[0, s] = out + raw[s].astype(jnp.float32) * (0.5 * held)
+            scale = scale + scales[t] * weights[s][t]
+        scale_ref[s] = scale
+        scale_ref[tiles + s] = jnp.full((width,), 0.5 * sum(weights[s]), jnp.float32)
+    store.wait()
     for n in range(CORES * pieces):
         for step in range(planes):
 
@@ -283,10 +336,14 @@
 
     for u in range(pieces):
         to_mate(u).wait_send()
-    for slot, peer in peers:
-        left_copy(slot, col, core, (row, peer), left_send.at[slot]).wait_send()
-    for c in range(ncol):
-        left_copy(0, c, core, mate, left_mate.at[c]).wait_send()
+    for t in range(tiles):
+        for d in along_x + along_y:
+            left_out((0, 0), d, t).wait_send()
+        for dy, dx in across:
+            source, move = ((0, dx), (dy, 0)) if t < half else ((dy, 0), (0, dx))
+            left_out(source, move, t).wait_send()
+        for c in range(ncol):
+            left_copy(c, t, core, mate, left_mate.at[c, t]).wait_send()
     flag_copy.wait_send()
     swap_copy.wait_send()
     for d in range(1, nrow):
@@ -298,11 +355,16 @@
     planes, depth, share = nrow // CORES, width // SPLIT, tiles // CORES
     pieces = share * SPLIT
     dma = pltpu.SemaphoreType.DMA
-    return pl.pallas_call(
+    squares, scale = pl.pallas_call(
         functools.partial(kernel, nrow, ncol),
-        out_shape=jax.ShapeDtypeStruct(flow_tiles.shape, jnp.float32),
-        in_specs=[pl.BlockSpec(memory_space=pl.ANY), pl.BlockSpec(memory_space=pl.ANY)],
-        out_specs=pl.BlockSpec(memory_space=pltpu.VMEM),
+        out_shape=(
+            jax.ShapeDtypeStruct(flow_tiles.shape, jnp.float32),
+            jax.ShapeDtypeStruct((2 * tiles, width), jnp.float32),
+        ),
+        in_specs=[pl.BlockSpec(memory_space=pltpu.HBM)] * 2,
+        out_specs=(
+            pl.BlockSpec(memory_space=pltpu.HBM), pl.BlockSpec(memory_space=pltpu.VMEM)
+        ),
         scratch_shapes=[
             pltpu.SMEM((1, tiles), jnp.int32),
             pltpu.VMEM((tiles, width, width), jnp.bfloat16),
@@ -312,16 +374,18 @@
             pltpu.VMEM((share, CORES, width, width), jnp.float32),
             pltpu.VMEM((share, width, width), jnp.float32),
             pltpu.VMEM((tiles, width, width), jnp.float32),
+            pltpu.VMEM((tiles, width, width), jnp.float32),
             pltpu.VMEM((CORES, tiles, width), jnp.float32),
             pltpu.VMEM((nrow, share, width), jnp.float32),
             dma((2,)),
+            dma,
             dma((planes, CORES * pieces)),
             dma((planes, CORES * pieces)),
             dma((pieces,)),
             dma((nrow, pieces)),
-            dma((ncol,)),
-            dma((CORES, ncol)),
-            dma((ncol,)),
+            dma((ncol, tiles)),
+            dma((CORES, ncol, tiles)),
+            dma((ncol, tiles)),
             dma((2,)),
             dma((2,)),
             dma((nrow,)),
@@ -332,6 +396,10 @@
         ),
         name="cluster_step",
     )(tile_cols, flow_tiles)
+    return (
+        flow_tiles.astype(jnp.float32) * scale[None, tiles:, None, :]
+        + squares * scale[None, :tiles, None, :]
+    )
 
 
 def solution(mesh):

time: 30.6 us -> 30.7 us (level)
  other arithmetic: 0 us -> 1.91 us
  local copies, waits for them, and re-layouts: 1.87 us -> 0.76 us
  Pallas kernels: 28.6 us -> 27.9 us
    add x0 -> x1, other arithmetic: none -> 1.91 us  [on_device(): flow_tiles.astype(jnp.float32) * scale[None, tiles:, None, :]]
    unnamed x1 -> x2, local copies, waits for them, and re-layouts: 1.87 us -> 0.01 us
    slice x0 -> x1, local copies, waits for them, and re-layouts: none -> 0.75 us  [on_device(): scale[None, tiles:, None, :]]
    pallas_call x1, Pallas kernels: 28.6 us -> 27.9 us  [on_device(): pl.pallas_call(functools.partial(kernel, nrow, ncol), out_shape=(jax.Shap...]
where the time goes in v3:
time: 30.7 us; the launch traced here: 30.5 us
  Pallas kernels  27.9 us (91%)
  other arithmetic  1.91 us (6%)
  local copies, waits for them, and re-layouts  0.76 us (2%)
    pallas_call x1, Pallas kernels, on_device(): pl.pallas_call(functools.partial(kernel, nrow, ncol), out_shape=(jax.Shap...  27.9 us
    add x1, other arithmetic, on_device(): flow_tiles.astype(jnp.float32) * scale[None, tiles:, None, :]  1.91 us
    slice x1, local copies, waits for them, and re-layouts, on_device(): scale[None, tiles:, None, :]  0.75 us

profile of v3, /device:TPU:0, one launch (start us, length us, event | category | flops | bytes accessed | tf_op | source)
XLA Modules:
  0.0 30.5 jit_solution(7689622070684876887)
XLA Ops:
  0.0 0.0 copy-start
  0.0 27.9 %cluster_step.1 = (f32[1,2,256,256]{3,2,1,0:T(8,128)}, f32[4,256]{1,0:T(4,128)}) custom-call(s32[1,2]{1,0:T(1,128)} %cols_hbm.1, bf16[1,2,256,256]{3,2,1,0:T(8,128)(2,1)} %flow_hbm.1), custom_call_target="tpu_custom_call" | custom-call | tf_op jit(solution)/shard_map/cluster_step/pallas_call | solution.py:358
  27.9 0.8 %fusion = (f32[2,256]{1,0:T(2,128)S(1)}, f32[2,256]{1,0:T(2,128)S(1)}) fusion(f32[4,256]{1,0:T(4,128)} %get-tuple-element.7), kind=kLoop, calls=%fused_computation.1 | loop fusion | bytes 8192 | tf_op jit(solution)/shard_map/slice | solution.py:400
  28.6 0.0 copy-done
  28.6 1.9 %multiply_add_fusion = f32[1,2,256,256]{3,2,1,0:T(8,128)} fusion(f32[1,2,256,256]{3,2,1,0:T(8,128)} %get-tuple-element.8, bf16[1,2,256,256]{3,2,1,0:T(8,128)(2,1)S(1)} %copy-done, f32[2,256]{1,0:T(2,128)S(1)} %get-tuple-element.10, f32[2,256]{1,0:T(2,128)S(1)} %get-tuple-element.9), kind=kLoop, calls=%fused_computation | loop fusion | flops 524288 | bytes 1314816 | tf_op jit(solution)/shard_map/add | solution.py:400
Async XLA Ops:
  0.0 28.6 %copy-start = (bf16[1,2,256,256]{3,2,1,0:T(8,128)(2,1)S(1)}, bf16[1,2,256,256]{3,2,1,0:T(8,128)(2,1)}, u32[]{:S(2)}) copy-start(bf16[1,2,256,256]{3,2,1,0:T(8,128)(2,1)} %flow_hbm.1) | copy-start | bytes 786436

commit v4 on v3

--- a/solution.py
+++ b/solution.py
@@ -25,9 +25,9 @@
 
 
 def kernel(
-    nrow, ncol, cols_hbm, flow_hbm, squares_ref, scale_ref,
-    cols, raw, own, blocks, left, acc, swap, result, placed, flags, sums,
-    in_sem, out_sem, up_send, dn_send, mate_send, recv, left_send, left_recv,
+    nrow, ncol, cols_hbm, flow_hbm, out_ref,
+    cols, raw, own, blocks, left, acc, swap, result, flags, sums,
+    in_sem, up_send, dn_send, mate_send, recv, left_send, left_recv,
     left_mate, flag_sem, swap_sem, sum_send, sum_recv,
 ):
     tiles, width = raw.shape[0], raw.shape[2]
@@ -292,37 +292,24 @@
         result[core * share + i] = mine * mine
     swap_copy.wait_recv()
 
-    weights = [
-        [(cols[0, s] == col + ncol * t).astype(jnp.float32) for t in range(tiles)]
-        for s in range(tiles)
-    ]
-    for s in range(tiles):
-        chosen = jnp.zeros((width, width), jnp.float32)
-        for t in range(tiles):
-            chosen = chosen + result[t] * weights[s][t]
-        placed[s] = chosen
-    store = pltpu.make_async_copy(placed, squares_ref.at[0], out_sem)
-    store.start()
-
     for d in range(1, nrow):
         other = (row + d) % nrow
         remote(
             sums.at[other], sums.at[other], sum_send.at[d], sum_recv.at[other], (other, col)
         ).wait_recv()
-    scales = []
-    for t in range(tiles):
-        total = sums[t // share, t % share]
-        for p in range(1, planes):
-            total = total + sums[p * CORES + t // share, t % share]
-        safe = jnp.where(total > 0, total, 1.0)
-        scales.append(jnp.float32(0.5 * nrow * width) / safe)
     for s in range(tiles):
-        scale = jnp.zeros((width,), jnp.float32)
+        out = jnp.zeros((width, width), jnp.float32)
+        held = jnp.float32(0)
         for t in range(tiles):
-            scale = scale + scales[t] * weights[s][t]
-        scale_ref[s] = scale
-        scale_ref[tiles + s] = jnp.full((width,), 0.5 * sum(weights[s]), jnp.float32)
-    store.wait()
+            w = (cols[0, s] == col + ncol * t).astype(jnp.float32)
+            held = held + w
+            total = sums[t // share, t % share]
+            for p in range(1, planes):
+                total = total + sums[p * CORES + t // share, t % share]
+            safe = jnp.where(total > 0, total, 1.0)
+            scale = jnp.float32(0.5 * nrow * width) / safe * w
+            out = out + result[t] * scale[None, :]
+        out_ref[0, s] = out + raw[s].astype(jnp.float32) * (0.5 * held)
     for n in range(CORES * pieces):
         for step in range(planes):
 
@@ -355,16 +342,11 @@
     planes, depth, share = nrow // CORES, width // SPLIT, tiles // CORES
     pieces = share * SPLIT
     dma = pltpu.SemaphoreType.DMA
-    squares, scale = pl.pallas_call(
+    return pl.pallas_call(
         functools.partial(kernel, nrow, ncol),
-        out_shape=(
-            jax.ShapeDtypeStruct(flow_tiles.shape, jnp.float32),
-            jax.ShapeDtypeStruct((2 * tiles, width), jnp.float32),
-        ),
+        out_shape=jax.ShapeDtypeStruct(flow_tiles.shape, jnp.float32),
         in_specs=[pl.BlockSpec(memory_space=pltpu.HBM)] * 2,
-        out_specs=(
-            pl.BlockSpec(memory_space=pltpu.HBM), pl.BlockSpec(memory_space=pltpu.VMEM)
-        ),
+        out_specs=pl.BlockSpec(memory_space=pltpu.VMEM),
         scratch_shapes=[
             pltpu.SMEM((1, tiles), jnp.int32),
             pltpu.VMEM((tiles, width, width), jnp.bfloat16),
@@ -374,11 +356,9 @@
             pltpu.VMEM((share, CORES, width, width), jnp.float32),
             pltpu.VMEM((share, width, width), jnp.float32),
             pltpu.VMEM((tiles, width, width), jnp.float32),
-            pltpu.VMEM((tiles, width, width), jnp.float32),
             pltpu.VMEM((CORES, tiles, width), jnp.float32),
             pltpu.VMEM((nrow, share, width), jnp.float32),
             dma((2,)),
-            dma,
             dma((planes, CORES * pieces)),
             dma((planes, CORES * pieces)),
             dma((pieces,)),
@@ -392,14 +372,10 @@
             dma((nrow,)),
         ],
         compiler_params=pltpu.CompilerParams(
-            collective_id=0, has_side_effects=True, vmem_limit_bytes=60 * 1024 * 1024
+            collective_id=0, has_side_effects=True, vmem_limit_bytes=24 * 1024 * 1024
         ),
         name="cluster_step",
     )(tile_cols, flow_tiles)
-    return (
-        flow_tiles.astype(jnp.float32) * scale[None, tiles:, None, :]
-        + squares * scale[None, :tiles, None, :]
-    )
 
 
 def solution(mesh):

time: 30.7 us -> 30 us (0.977)
  other arithmetic: 1.91 us -> 0 us
  local copies, waits for them, and re-layouts: 0.76 us -> 2.4 us
  Pallas kernels: 27.9 us -> 27.4 us
    unnamed x2 -> x5, local copies, waits for them, and re-layouts: 0.01 us -> 2.4 us
    add x1 -> x0, other arithmetic: 1.91 us -> none  [on_device(): flow_tiles.astype(jnp.float32) * scale[None, tiles:, None, :]]
    slice x1 -> x0, local copies, waits for them, and re-layouts: 0.75 us -> none  [on_device(): scale[None, tiles:, None, :]]
    pallas_call x1, Pallas kernels: 27.9 us -> 27.4 us  [on_device(): pl.pallas_call(functools.partial(kernel, nrow, ncol), out_shape=jax.Shape...]
where the time goes in v4:
time: 30 us; the launch traced here: 29.8 us
  Pallas kernels  27.4 us (91%)
  local copies, waits for them, and re-layouts  2.4 us (8%)
    pallas_call x1, Pallas kernels, on_device(): pl.pallas_call(functools.partial(kernel, nrow, ncol), out_shape=jax.Shape...  27.4 us
    unnamed x5, local copies, waits for them, and re-layouts  2.4 us

profile of v4, /device:TPU:0, one launch (start us, length us, event | category | flops | bytes accessed | tf_op | source)
XLA Modules:
  0.0 29.8 jit_solution(9763162112491246535)
XLA Ops:
  0.0 0.0 copy-start
  0.0 0.9 %copy-done = bf16[1,2,256,256]{3,2,1,0:T(8,128)(2,1)S(1)} copy-done((bf16[1,2,256,256]{3,2,1,0:T(8,128)(2,1)S(1)}, bf16[1,2,256,256]{3,2,1,0:T(8,128)(2,1)}, u32[]{:S(2)}) %copy-start) | copy-done | bytes 262168
  1.0 0.0 copy-start.1
  1.0 0.7 %copy-done.1 = s32[1,2]{1,0:T(1,128)S(1)} copy-done((s32[1,2]{1,0:T(1,128)S(1)}, s32[1,2]{1,0:T(1,128)}, u32[]{:S(2)}) %copy-start.1) | copy-done | bytes 32
  1.6 27.4 %cluster_step.1 = f32[1,2,256,256]{3,2,1,0:T(8,128)S(1)} custom-call(s32[1,2]{1,0:T(1,128)S(1)} %copy-done.1, bf16[1,2,256,256]{3,2,1,0:T(8,128)(2,1)S(1)} %copy-done), custom_call_target="tpu_custom_call" | custom-call | tf_op jit(solution)/shard_map/cluster_step/pallas_call | solution.py:345
  29.0 0.8 %copy.4 = f32[1,2,256,256]{3,2,1,0:T(8,128)} copy(f32[1,2,256,256]{3,2,1,0:T(8,128)S(1)} %cluster_step.1) | data formatting | bytes 1048576
Async XLA Ops:
  0.0 0.9 %copy-start = (bf16[1,2,256,256]{3,2,1,0:T(8,128)(2,1)S(1)}, bf16[1,2,256,256]{3,2,1,0:T(8,128)(2,1)}, u32[]{:S(2)}) copy-start(bf16[1,2,256,256]{3,2,1,0:T(8,128)(2,1)} %flow_hbm.1) | copy-start | bytes 786436
  1.0 0.7 %copy-start.1 = (s32[1,2]{1,0:T(1,128)S(1)}, s32[1,2]{1,0:T(1,128)}, u32[]{:S(2)}) copy-start(s32[1,2]{1,0:T(1,128)} %cols_hbm.1) | copy-start | bytes 28
